TPU v7x, 512 devices: a whole 4x8x8 slice. The times are simulated.
512 devices in a mesh: dom: 512 (over z, x, y, core).
Axes of the slice: x: 4, y: 8, z: 8, core: 2. Of those that a mesh axis runs over, the one named last changes fastest.
Arguments:
- tracers: float32 [20, 8, 524288], P(None, None, 'dom'), may hold values from -6 to 6
- mass_flux: float32 [3, 8, 524288], P(None, None, 'dom'), may hold values from -6 to 6
- lsq_coeff: float32 [2, 3, 524288], P(None, None, 'dom'), may hold values from -3 to 3
- own_offset: float32 [2, 3, 8, 524288], P(None, None, None, 'dom'), may hold values from -1.5 to 1.5
- far_offset: float32 [2, 3, 8, 524288], P(None, None, None, 'dom'), may hold values from -1.5 to 1.5
- inv_mass: float32 [8, 524288], P(None, 'dom'), may hold values from 0.25 to 1
- neighbour: int32 [3, 524288], P(None, 'dom'), may hold values from 0 to 1791, as said below
- send_cells: int32 [6, 65536], P(None, 'dom'), may hold values from 0 to 1023, as said below
Outputs:
- updated: float32 [20, 8, 524288], P(None, None, 'dom')
Inputs may be any that keep to these rules, and one draw needn't show every extreme that they name: For each domain, entries index its 1024 own cells followed by 6 received blocks of 128 slots; every referenced received slot holds a real cell of the sending domain, the unused tail of a block is never referenced, and for every neighbour slot some domain references a block in full. `send_cells`: each block of 128 entries (one sending domain, one neighbour slot) lists distinct own cells of the sending domain, as local indices.
All inputs are finite; a program needn't handle non-finite values.
Results may differ from a plain program's by a relative error of at most 0.0003.
Values sent between devices are 32-bit elements; how exact they have to be, the bound alone decides.
A program may use at most 64 MiB of HBM per device.

v0:
```python
import jax
import jax.numpy as jnp
from jax import lax
from jax.sharding import PartitionSpec as P


def passed_along(block, axis, distance):
    devices = range(lax.axis_size(axis))
    route = [((i - distance) % len(devices), i) for i in devices]
    return lax.ppermute(block, axis, route)


def peer_shift(peer_slot):
    return (peer_slot // 2 + 1) * (1 - 2 * (peer_slot % 2))


def spread(blocks, halo_kind):
    block_count = len(blocks)
    arrived = [None] * block_count
    for peer_slot in range(block_count):
        if halo_kind == "values":
            arrived[peer_slot] = passed_along(blocks[peer_slot], "dom", peer_shift(peer_slot))
        else:
            arrived[peer_slot] = passed_along(blocks[peer_slot], "dom", peer_shift(peer_slot))
    return arrived


def cut_blocks(sent, count, width):
    return [sent[:, slot * width : (slot + 1) * width] for slot in range(count)]


def on_device(
    tracers, mass_flux, lsq_coeff, own_offset, far_offset, inv_mass, neighbour, send_cells
):
    tracer_count, level_count, cell_count = tracers.shape
    row_count = tracer_count * level_count
    peer_count, halo_width = send_cells.shape
    send_flat = send_cells.reshape(peer_count * halo_width)
    near_flat = neighbour.reshape(3 * cell_count)
    flat = tracers.reshape(row_count, cell_count)
    value_sent = jnp.take(flat, send_flat, axis=1, mode="clip")
    extended = jnp.concatenate(
        [flat] + spread(cut_blocks(value_sent, peer_count, halo_width), "values"), axis=1
    )
    beside_all = jnp.take(extended, near_flat, axis=1, mode="clip")
    beside = [
        beside_all[:, edge_slot * cell_count : (edge_slot + 1) * cell_count]
        for edge_slot in range(3)
    ]
    parts = []
    for comp in range(2):
        total = None
        for edge_slot in range(3):
            summand = lsq_coeff[comp, edge_slot][None, :] * (beside[edge_slot] - flat)
            total = summand if total is None else total + summand
        parts.append(total)
    grad_flat = jnp.concatenate(parts, axis=0)
    grad_sent = jnp.take(grad_flat, send_flat, axis=1, mode="clip")
    grad_extended = jnp.concatenate(
        [grad_flat] + spread(cut_blocks(grad_sent, peer_count, halo_width), "gradients"), axis=1
    )
    far_all = jnp.take(grad_extended, near_flat, axis=1, mode="clip")
    shape_three = (tracer_count, level_count, cell_count)
    grad_first = parts[0].reshape(shape_three)
    grad_second = parts[1].reshape(shape_three)
    outflow = jnp.zeros_like(tracers)
    for edge_slot in range(3):
        far_value = beside[edge_slot].reshape(shape_three)
        far_block = far_all[:, edge_slot * cell_count : (edge_slot + 1) * cell_count]
        far_first = far_block[:row_count].reshape(shape_three)
        far_second = far_block[row_count:].reshape(shape_three)
        own_face = (
            tracers + grad_first * own_offset[0, edge_slot] + grad_second * own_offset[1, edge_slot]
        )
        far_face = (
            far_value + far_first * far_offset[0, edge_slot] + far_second * far_offset[1, edge_slot]
        )
        side_flux = mass_flux[edge_slot]
        face_value = jnp.where(side_flux > 0, own_face, far_face)
        face_value = jnp.clip(
            face_value, jnp.minimum(tracers, far_value), jnp.maximum(tracers, far_value)
        )
        outflow = outflow + side_flux * face_value
    return tracers - inv_mass * outflow


def solution(mesh):
    placed = (
        P(None, None, "dom"),
        P(None, None, "dom"),
        P(None, None, "dom"),
        P(None, None, None, "dom"),
        P(None, None, None, "dom"),
        P(None, "dom"),
        P(None, "dom"),
        P(None, "dom"),
    )
    return jax.shard_map(
        on_device, mesh=mesh, in_specs=placed, out_specs=P(None, None, "dom"), check_vma=False
    )
```

profile of v0, /device:TPU:247, one launch (start us, length us, event | category | flops | bytes accessed | tf_op | source)
XLA Modules:
  0.0 145.6 jit_solution(3735102446030123631)
XLA Ops:
  0.0 1.4 copy.48
  2.1 2.1 %gather_fusion = f32[768,160]{1,0:T(8,128)S(1)} fusion(f32[160,1024]{0,1:T(8,128)S(1)} %copy.48, s32[1024]{0:T(1024)S(1)} %pad_clamp_fusion), kind=kCustom, calls=%fused_computation | custom fusion | bytes 986112 | tf_op jit(solution)/shard_map/jit(_take)/gather | solution.py:41
  5.1 2.9 %collective-permute-start = (f32[160,128]{0,1:T(8,128)}, f32[160,128]{0,1:T(8,128)}, u32[]{:S(2)}, u32[]{:S(2)}) collective-permute-start(f32[160,128]{0,1:T(8,128)} %get-tuple-element.26), channel_id=1, source_target_pairs={{511,0},{0,1},{1,2},{2,3},{3,4},{4,5},{5,6},{6,7},{7,8},{8,9},{9,1... | collective-permute-start | bytes 245768 | tf_op jit(solution)/shard_map/ppermute | solution.py:10
  8.0 1.9 %collective-permute-start.1 = (f32[160,128]{0,1:T(8,128)}, f32[160,128]{0,1:T(8,128)}, u32[]{:S(2)}, u32[]{:S(2)}) collective-permute-start(f32[160,128]{0,1:T(8,128)} %get-tuple-element.25), channel_id=1, source_target_pairs={{1,0},{2,1},{3,2},{4,3},{5,4},{6,5},{7,6},{8,7},{9,8},{10,9},{11,1... | collective-permute-start | bytes 245768 | tf_op jit(solution)/shard_map/ppermute | solution.py:10
  9.9 4.3 %collective-permute-start.2 = (f32[160,128]{0,1:T(8,128)}, f32[160,128]{0,1:T(8,128)}, u32[]{:S(2)}, u32[]{:S(2)}) collective-permute-start(f32[160,128]{0,1:T(8,128)} %get-tuple-element.24), channel_id=1, source_target_pairs={{510,0},{511,1},{0,2},{1,3},{2,4},{3,5},{4,6},{5,7},{6,8},{7,9},{8... | collective-permute-start | bytes 245768 | tf_op jit(solution)/shard_map/ppermute | solution.py:10
  14.2 1.9 %collective-permute-start.3 = (f32[160,128]{0,1:T(8,128)}, f32[160,128]{0,1:T(8,128)}, u32[]{:S(2)}, u32[]{:S(2)}) collective-permute-start(f32[160,128]{0,1:T(8,128)} %get-tuple-element.23), channel_id=1, source_target_pairs={{2,0},{3,1},{4,2},{5,3},{6,4},{7,5},{8,6},{9,7},{10,8},{11,9},{12,... | collective-permute-start | bytes 245768 | tf_op jit(solution)/shard_map/ppermute | solution.py:10
  16.2 16.2 %collective-permute-start.4 = (f32[160,128]{0,1:T(8,128)}, f32[160,128]{0,1:T(8,128)}, u32[]{:S(2)}, u32[]{:S(2)}) collective-permute-start(f32[160,128]{0,1:T(8,128)} %get-tuple-element.22), channel_id=1, source_target_pairs={{509,0},{510,1},{511,2},{0,3},{1,4},{2,5},{3,6},{4,7},{5,8},{6,9},... | collective-permute-start | bytes 245768 | tf_op jit(solution)/shard_map/ppermute | solution.py:10
  34.6 1.9 %collective-permute-start.5 = (f32[160,128]{0,1:T(8,128)S(1)}, f32[160,128]{0,1:T(8,128)S(1)}, u32[]{:S(2)}, u32[]{:S(2)}) collective-permute-start(f32[160,128]{0,1:T(8,128)S(1)} %get-tuple-element.21), channel_id=1, source_target_pairs={{3,0},{4,1},{5,2},{6,3},{7,4},{8,5},{9,6},{10,7},{11,8},{12,9},{13... | collective-permute-start | bytes 245768 | tf_op jit(solution)/shard_map/ppermute | solution.py:10
  36.5 0.9 constant_dynamic-update-slice_fusion.5
  37.5 0.9 constant_dynamic-update-slice_fusion.4
  41.2 6.1 %collective-permute-done.5 = f32[160,128]{0,1:T(8,128)S(1)} collective-permute-done((f32[160,128]{0,1:T(8,128)S(1)}, f32[160,128]{0,1:T(8,128)S(1)}, u32[]{:S(2)}, u32[]{:S(2)}) %collective-permute-start.5) | collective-permute-done | bytes 81952 | tf_op jit(solution)/shard_map/ppermute | solution.py:10
  47.2 12.4 %gather_fusion.1 = f32[3072,160]{1,0:T(8,128)} fusion(f32[160,1792]{0,1:T(8,128)S(1)} %constant_dynamic-update-slice_fusion, s32[3072]{0:T(1024)S(1)} %broadcast_clamp_fusion), kind=kCustom, calls=%fused_computation.1 | custom fusion | bytes 3944448 | tf_op jit(solution)/shard_map/jit(_take)/gather | solution.py:45
  59.7 2.4 %copy.49 = f32[3072,160]{0,1:T(8,128)S(1)} copy(f32[3072,160]{1,0:T(8,128)} %gather_fusion.1) | data formatting | bytes 3932160 | tf_op jit(solution)/shard_map/jit(_take)/gather | solution.py:45
  63.4 1.5 %pad_maximum_fusion = (f32[320,1024]{1,0:T(8,128)S(1)}, f32[320,1792]{1,0:T(8,128)}) fusion(f32[160,1024]{1,0:T(8,128)S(1)} %get-tuple-element.12, f32[160,1024]{1,0:T(8,128)S(1)} %get-tuple-element.11), kind=kLoop, calls=%fused_computation.4 | loop fusion | flops 327679 | bytes 3932160 | tf_op jit(solution)/shard_map/concatenate | solution.py:57
  65.3 2.1 %gather_fusion.2 = f32[768,320]{1,0:T(8,128)S(1)} fusion(f32[320,1024]{0,1:T(8,128)S(1)} %copy.50, s32[1024]{0:T(1024)S(1)} %pad_clamp_fusion), kind=kCustom, calls=%fused_computation.2 | custom fusion | bytes 1969152 | tf_op jit(solution)/shard_map/jit(_take)/gather | solution.py:58
  67.9 1.9 %collective-permute-start.6 = (f32[320,128]{1,0:T(8,128)S(1)}, f32[320,128]{1,0:T(8,128)S(1)}, u32[]{:S(2)}, u32[]{:S(2)}) collective-permute-start(f32[320,128]{1,0:T(8,128)S(1)} %get-tuple-element.20), channel_id=1, source_target_pairs={{511,0},{0,1},{1,2},{2,3},{3,4},{4,5},{5,6},{6,7},{7,8},{8,9},{9,1... | collective-permute-start | bytes 491528 | tf_op jit(solution)/shard_map/ppermute | solution.py:10
  69.8 2.4 %collective-permute-start.7 = (f32[320,128]{1,0:T(8,128)S(1)}, f32[320,128]{1,0:T(8,128)S(1)}, u32[]{:S(2)}, u32[]{:S(2)}) collective-permute-start(f32[320,128]{1,0:T(8,128)S(1)} %get-tuple-element.19), channel_id=1, source_target_pairs={{1,0},{2,1},{3,2},{4,3},{5,4},{6,5},{7,6},{8,7},{9,8},{10,9},{11,1... | collective-permute-start | bytes 491528 | tf_op jit(solution)/shard_map/ppermute | solution.py:10
  72.9 3.7 %collective-permute-start.8 = (f32[320,128]{1,0:T(8,128)S(1)}, f32[320,128]{1,0:T(8,128)S(1)}, u32[]{:S(2)}, u32[]{:S(2)}) collective-permute-start(f32[320,128]{1,0:T(8,128)S(1)} %get-tuple-element.18), channel_id=1, source_target_pairs={{510,0},{511,1},{0,2},{1,3},{2,4},{3,5},{4,6},{5,7},{6,8},{7,9},{8... | collective-permute-start | bytes 491528 | tf_op jit(solution)/shard_map/ppermute | solution.py:10
  76.6 1.9 %collective-permute-start.9 = (f32[320,128]{1,0:T(8,128)S(1)}, f32[320,128]{1,0:T(8,128)S(1)}, u32[]{:S(2)}, u32[]{:S(2)}) collective-permute-start(f32[320,128]{1,0:T(8,128)S(1)} %get-tuple-element.17), channel_id=1, source_target_pairs={{2,0},{3,1},{4,2},{5,3},{6,4},{7,5},{8,6},{9,7},{10,8},{11,9},{12,... | collective-permute-start | bytes 491528 | tf_op jit(solution)/shard_map/ppermute | solution.py:10
  78.5 16.2 %collective-permute-start.10 = (f32[320,128]{1,0:T(8,128)S(1)}, f32[320,128]{1,0:T(8,128)S(1)}, u32[]{:S(2)}, u32[]{:S(2)}) collective-permute-start(f32[320,128]{1,0:T(8,128)S(1)} %get-tuple-element.16), channel_id=1, source_target_pairs={{509,0},{510,1},{511,2},{0,3},{1,4},{2,5},{3,6},{4,7},{5,8},{6,9},... | collective-permute-start | bytes 491528 | tf_op jit(solution)/shard_map/ppermute | solution.py:10
  94.8 1.9 %collective-permute-start.11 = (f32[320,128]{1,0:T(8,128)S(1)}, f32[320,128]{1,0:T(8,128)S(1)}, u32[]{:S(2)}, u32[]{:S(2)}) collective-permute-start(f32[320,128]{1,0:T(8,128)S(1)} %get-tuple-element.15), channel_id=1, source_target_pairs={{3,0},{4,1},{5,2},{6,3},{7,4},{8,5},{9,6},{10,7},{11,8},{12,9},{13... | collective-permute-start | bytes 491528 | tf_op jit(solution)/shard_map/ppermute | solution.py:10
  100.3 7.5 %collective-permute-done.11 = f32[320,128]{1,0:T(8,128)S(1)} collective-permute-done((f32[320,128]{1,0:T(8,128)S(1)}, f32[320,128]{1,0:T(8,128)S(1)}, u32[]{:S(2)}, u32[]{:S(2)}) %collective-permute-start.11) | collective-permute-done | bytes 163872 | tf_op jit(solution)/shard_map/ppermute | solution.py:10
  108.5 2.1 %copy.52 = f32[320,1792]{0,1:T(8,128)S(1)} copy(f32[320,1792]{1,0:T(8,128)} %constant_dynamic-update-slice_fusion.7) | data formatting | bytes 4587520 | tf_op jit(solution)/shard_map/concatenate | solution.py:59
  110.6 12.6 %gather_fusion.3 = f32[3072,320]{1,0:T(8,128)} fusion(f32[320,1792]{0,1:T(8,128)S(1)} %copy.52, s32[3072]{0:T(1024)S(1)} %broadcast_clamp_fusion), kind=kCustom, calls=%fused_computation.3 | custom fusion | bytes 7876608 | tf_op jit(solution)/shard_map/jit(_take)/gather | solution.py:62
  123.2 5.7 %fusion.28 = (f32[160,1024]{0,1:T(8,128)}, f32[160,1024]{0,1:T(8,128)}, f32[160,1024]{0,1:T(8,128)S(1)}, f32[160,1024]{0,1:T(8,128)S(1)}, f32[160,1024]{0,1:T(8,128)}, /*index=5*/f32[160,1024]{0,1:T(8,128)}) fusion(f32[320,3072]{0,1:T(8,128)} %bitcast.172), kind=kLoop, calls=%fused_computation.90 | loop fusion | bytes 7864320 | tf_op jit(solution)/shard_map/slice | solution.py:70
  128.9 2.4 %copy.53 = f32[160,1024]{1,0:T(8,128)} copy(f32[160,1024]{0,1:T(8,128)} %get-tuple-element.5) | data formatting | bytes 1310720 | tf_op jit(solution)/shard_map/slice | solution.py:70
  131.3 2.4 %copy.54 = f32[160,1024]{1,0:T(8,128)} copy(f32[160,1024]{0,1:T(8,128)} %get-tuple-element.9) | data formatting | bytes 1310720 | tf_op jit(solution)/shard_map/slice | solution.py:71
  133.7 1.2 copy.55
  134.9 1.2 copy.56
  136.1 2.5 %copy.57 = f32[160,1024]{1,0:T(8,128)} copy(f32[160,1024]{0,1:T(8,128)} %get-tuple-element.6) | data formatting | bytes 1310720 | tf_op jit(solution)/shard_map/slice | solution.py:70
  138.7 2.4 %copy.58 = f32[160,1024]{1,0:T(8,128)} copy(f32[160,1024]{0,1:T(8,128)} %get-tuple-element.10) | data formatting | bytes 1310720 | tf_op jit(solution)/shard_map/slice | solution.py:71
  141.2 4.4 %fusion.7 = f32[20,8,1024]{2,1,0:T(8,128)} fusion(f32[20,8,1024]{2,1,0:T(8,128)S(1)} %copy-done.2, f32[160,1024]{1,0:T(8,128)} %copy.58, f32[160,1024]{1,0:T(8,128)} %copy.57, f32[160,1024]{1,0:T(8,128)} %copy.56, f32[160,1024]{1,0:T(8,128)} %copy.55, f32[160,1024]{1,0:T(8,128)} %copy.54, f32[160,1024]{1,0:T(8,128)} %copy.53, f32[160,1024]{1,0:T(8,128)} %copy-done.5, ...), kind=kLoop, calls=%fused_computation.13 | loop fusion | flops 7536640 | bytes 9068544 | tf_op jit(solution)/shard_map/sub | solution.py:84
  (89 shorter events, 13.5 us)
Async XLA Ops:
  2.1 30.3 %copy-start.21 = (s32[3,1024]{1,0:T(4,128)S(1)}, s32[3,1024]{1,0:T(4,128)}, u32[]{:S(2)}) copy-start(s32[3,1024]{1,0:T(4,128)} %param.14) | copy-start | bytes 36868
  2.1 30.3 %copy-start.20 = (f32[2,3,1024]{2,0,1:T(2,128)S(1)}, f32[2,3,1024]{2,0,1:T(2,128)}, u32[]{:S(2)}) copy-start(f32[2,3,1024]{2,0,1:T(2,128)} %param.10) | copy-start | bytes 73732
  2.1 31.0 %copy-start.6 = (f32[3,8,1024]{2,1,0:T(8,128)S(1)}, f32[3,8,1024]{2,1,0:T(8,128)}, u32[]{:S(2)}) copy-start(f32[3,8,1024]{2,1,0:T(8,128)} %param.9) | copy-start | bytes 294916
  4.2 29.5 %copy-start.8 = (f32[2,3,8,1024]{3,2,1,0:T(8,128)S(1)}, f32[2,3,8,1024]{3,2,1,0:T(8,128)}, u32[]{:S(2)}) copy-start(f32[2,3,8,1024]{3,2,1,0:T(8,128)} %param.12) | copy-start | bytes 589828
  4.3 29.5 %copy-start.9 = (f32[2,3,8,1024]{3,2,1,0:T(8,128)S(1)}, f32[2,3,8,1024]{3,2,1,0:T(8,128)}, u32[]{:S(2)}) copy-start(f32[2,3,8,1024]{3,2,1,0:T(8,128)} %param.11) | copy-start | bytes 589828
  5.1 29.5 %collective-permute-start = (f32[160,128]{0,1:T(8,128)}, f32[160,128]{0,1:T(8,128)}, u32[]{:S(2)}, u32[]{:S(2)}) collective-permute-start(f32[160,128]{0,1:T(8,128)} %get-tuple-element.26), channel_id=1, source_target_pairs={{511,0},{0,1},{1,2},{2,3},{3,4},{4,5},{5,6},{6,7},{7,8},{8,9},{9,1... | collective-permute-start | bytes 245768 | tf_op jit(solution)/shard_map/ppermute | solution.py:10
  8.0 29.5 %collective-permute-start.1 = (f32[160,128]{0,1:T(8,128)}, f32[160,128]{0,1:T(8,128)}, u32[]{:S(2)}, u32[]{:S(2)}) collective-permute-start(f32[160,128]{0,1:T(8,128)} %get-tuple-element.25), channel_id=1, source_target_pairs={{1,0},{2,1},{3,2},{4,3},{5,4},{6,5},{7,6},{8,7},{9,8},{10,9},{11,1... | collective-permute-start | bytes 245768 | tf_op jit(solution)/shard_map/ppermute | solution.py:10
  9.9 28.5 %collective-permute-start.2 = (f32[160,128]{0,1:T(8,128)}, f32[160,128]{0,1:T(8,128)}, u32[]{:S(2)}, u32[]{:S(2)}) collective-permute-start(f32[160,128]{0,1:T(8,128)} %get-tuple-element.24), channel_id=1, source_target_pairs={{510,0},{511,1},{0,2},{1,3},{2,4},{3,5},{4,6},{5,7},{6,8},{7,9},{8... | collective-permute-start | bytes 245768 | tf_op jit(solution)/shard_map/ppermute | solution.py:10
  14.2 25.1 %collective-permute-start.3 = (f32[160,128]{0,1:T(8,128)}, f32[160,128]{0,1:T(8,128)}, u32[]{:S(2)}, u32[]{:S(2)}) collective-permute-start(f32[160,128]{0,1:T(8,128)} %get-tuple-element.23), channel_id=1, source_target_pairs={{2,0},{3,1},{4,2},{5,3},{6,4},{7,5},{8,6},{9,7},{10,8},{11,9},{12,... | collective-permute-start | bytes 245768 | tf_op jit(solution)/shard_map/ppermute | solution.py:10
  16.2 24.1 %collective-permute-start.4 = (f32[160,128]{0,1:T(8,128)}, f32[160,128]{0,1:T(8,128)}, u32[]{:S(2)}, u32[]{:S(2)}) collective-permute-start(f32[160,128]{0,1:T(8,128)} %get-tuple-element.22), channel_id=1, source_target_pairs={{509,0},{510,1},{511,2},{0,3},{1,4},{2,5},{3,6},{4,7},{5,8},{6,9},... | collective-permute-start | bytes 245768 | tf_op jit(solution)/shard_map/ppermute | solution.py:10
  34.6 12.6 %collective-permute-start.5 = (f32[160,128]{0,1:T(8,128)S(1)}, f32[160,128]{0,1:T(8,128)S(1)}, u32[]{:S(2)}, u32[]{:S(2)}) collective-permute-start(f32[160,128]{0,1:T(8,128)S(1)} %get-tuple-element.21), channel_id=1, source_target_pairs={{3,0},{4,1},{5,2},{6,3},{7,4},{8,5},{9,6},{10,7},{11,8},{12,9},{13... | collective-permute-start | bytes 245768 | tf_op jit(solution)/shard_map/ppermute | solution.py:10
  59.6 2.5 %copy-start.25 = (f32[1,1,1024]{2,0,1:T(1,128)S(1)}, f32[1,1,1024]{2,0,1:T(1,128)}, u32[]{:S(2)}) copy-start(f32[1,1,1024]{2,0,1:T(1,128)} %get-tuple-element.48) | copy-start | bytes 12292
  59.7 2.5 %copy-start.26 = (f32[1,1,1024]{2,0,1:T(1,128)S(1)}, f32[1,1,1024]{2,0,1:T(1,128)}, u32[]{:S(2)}) copy-start(f32[1,1,1024]{2,0,1:T(1,128)} %get-tuple-element.49) | copy-start | bytes 12292
  67.5 4.8 %copy-start.7 = (f32[3,8,1024]{2,1,0:T(8,128)S(1)}, f32[3,8,1024]{2,1,0:T(8,128)}, u32[]{:S(2)}) copy-start(f32[3,8,1024]{2,1,0:T(8,128)} %param.9) | copy-start | bytes 294916
  67.9 26.9 %collective-permute-start.6 = (f32[320,128]{1,0:T(8,128)S(1)}, f32[320,128]{1,0:T(8,128)S(1)}, u32[]{:S(2)}, u32[]{:S(2)}) collective-permute-start(f32[320,128]{1,0:T(8,128)S(1)} %get-tuple-element.20), channel_id=1, source_target_pairs={{511,0},{0,1},{1,2},{2,3},{3,4},{4,5},{5,6},{6,7},{7,8},{8,9},{9,1... | collective-permute-start | bytes 491528 | tf_op jit(solution)/shard_map/ppermute | solution.py:10
  69.8 27.6 %collective-permute-start.7 = (f32[320,128]{1,0:T(8,128)S(1)}, f32[320,128]{1,0:T(8,128)S(1)}, u32[]{:S(2)}, u32[]{:S(2)}) collective-permute-start(f32[320,128]{1,0:T(8,128)S(1)} %get-tuple-element.19), channel_id=1, source_target_pairs={{1,0},{2,1},{3,2},{4,3},{5,4},{6,5},{7,6},{8,7},{9,8},{10,9},{11,1... | collective-permute-start | bytes 491528 | tf_op jit(solution)/shard_map/ppermute | solution.py:10
  72.9 25.2 %collective-permute-start.8 = (f32[320,128]{1,0:T(8,128)S(1)}, f32[320,128]{1,0:T(8,128)S(1)}, u32[]{:S(2)}, u32[]{:S(2)}) collective-permute-start(f32[320,128]{1,0:T(8,128)S(1)} %get-tuple-element.18), channel_id=1, source_target_pairs={{510,0},{511,1},{0,2},{1,3},{2,4},{3,5},{4,6},{5,7},{6,8},{7,9},{8... | collective-permute-start | bytes 491528 | tf_op jit(solution)/shard_map/ppermute | solution.py:10
  76.6 22.2 %collective-permute-start.9 = (f32[320,128]{1,0:T(8,128)S(1)}, f32[320,128]{1,0:T(8,128)S(1)}, u32[]{:S(2)}, u32[]{:S(2)}) collective-permute-start(f32[320,128]{1,0:T(8,128)S(1)} %get-tuple-element.17), channel_id=1, source_target_pairs={{2,0},{3,1},{4,2},{5,3},{6,4},{7,5},{8,6},{9,7},{10,8},{11,9},{12,... | collective-permute-start | bytes 491528 | tf_op jit(solution)/shard_map/ppermute | solution.py:10
  78.5 21.0 %collective-permute-start.10 = (f32[320,128]{1,0:T(8,128)S(1)}, f32[320,128]{1,0:T(8,128)S(1)}, u32[]{:S(2)}, u32[]{:S(2)}) collective-permute-start(f32[320,128]{1,0:T(8,128)S(1)} %get-tuple-element.16), channel_id=1, source_target_pairs={{509,0},{510,1},{511,2},{0,3},{1,4},{2,5},{3,6},{4,7},{5,8},{6,9},... | collective-permute-start | bytes 491528 | tf_op jit(solution)/shard_map/ppermute | solution.py:10
  94.8 13.0 %collective-permute-start.11 = (f32[320,128]{1,0:T(8,128)S(1)}, f32[320,128]{1,0:T(8,128)S(1)}, u32[]{:S(2)}, u32[]{:S(2)}) collective-permute-start(f32[320,128]{1,0:T(8,128)S(1)} %get-tuple-element.15), channel_id=1, source_target_pairs={{3,0},{4,1},{5,2},{6,3},{7,4},{8,5},{9,6},{10,7},{11,8},{12,9},{13... | collective-permute-start | bytes 491528 | tf_op jit(solution)/shard_map/ppermute | solution.py:10
  136.0 5.0 %copy-start.1 = (f32[3072,160]{0,1:T(8,128)S(1)}, f32[3072,160]{0,1:T(8,128)}, u32[]{:S(2)}) copy-start(f32[3072,160]{0,1:T(8,128)} %copy-done) | copy-start | bytes 5898244
  136.0 5.0 %copy-start.4 = (f32[160,1024]{1,0:T(8,128)S(1)}, f32[160,1024]{1,0:T(8,128)}, u32[]{:S(2)}) copy-start(f32[160,1024]{1,0:T(8,128)} %copy-done.3) | copy-start | bytes 1966084
  136.0 5.0 %copy-start.10 = (f32[8,1024]{1,0:T(8,128)S(1)}, f32[8,1024]{1,0:T(8,128)}, u32[]{:S(2)}) copy-start(f32[8,1024]{1,0:T(8,128)} %get-tuple-element.33) | copy-start | bytes 98308
  136.0 5.0 %copy-start.11 = (f32[8,1024]{1,0:T(8,128)S(1)}, f32[8,1024]{1,0:T(8,128)}, u32[]{:S(2)}) copy-start(f32[8,1024]{1,0:T(8,128)} %get-tuple-element.34) | copy-start | bytes 98308
  136.1 5.1 %copy-start.12 = (f32[8,1024]{1,0:T(8,128)S(1)}, f32[8,1024]{1,0:T(8,128)}, u32[]{:S(2)}) copy-start(f32[8,1024]{1,0:T(8,128)} %get-tuple-element.35) | copy-start | bytes 98308
  136.1 5.1 %copy-start.13 = (f32[8,1024]{1,0:T(8,128)S(1)}, f32[8,1024]{1,0:T(8,128)}, u32[]{:S(2)}) copy-start(f32[8,1024]{1,0:T(8,128)} %get-tuple-element.36) | copy-start | bytes 98308
  136.1 5.1 %copy-start.14 = (f32[8,1024]{1,0:T(8,128)S(1)}, f32[8,1024]{1,0:T(8,128)}, u32[]{:S(2)}) copy-start(f32[8,1024]{1,0:T(8,128)} %get-tuple-element.37) | copy-start | bytes 98308
  136.1 5.1 %copy-start.15 = (f32[8,1024]{1,0:T(8,128)S(1)}, f32[8,1024]{1,0:T(8,128)}, u32[]{:S(2)}) copy-start(f32[8,1024]{1,0:T(8,128)} %get-tuple-element.38) | copy-start | bytes 98308
  136.1 5.1 %copy-start.16 = (f32[8,1024]{1,0:T(8,128)S(1)}, f32[8,1024]{1,0:T(8,128)}, u32[]{:S(2)}) copy-start(f32[8,1024]{1,0:T(8,128)} %get-tuple-element.51) | copy-start | bytes 98308
  136.1 5.1 %copy-start.17 = (f32[8,1024]{1,0:T(8,128)S(1)}, f32[8,1024]{1,0:T(8,128)}, u32[]{:S(2)}) copy-start(f32[8,1024]{1,0:T(8,128)} %get-tuple-element.52) | copy-start | bytes 98308
  136.1 5.1 %copy-start.18 = (pred[8,1024]{1,0:T(8,128)(4,1)S(1)}, pred[8,1024]{1,0:T(8,128)(4,1)}, u32[]{:S(2)}) copy-start(pred[8,1024]{1,0:T(8,128)(4,1)} %get-tuple-element.39) | copy-start | bytes 24580
  136.1 5.1 %copy-start.19 = (pred[8,1024]{1,0:T(8,128)(4,1)S(1)}, pred[8,1024]{1,0:T(8,128)(4,1)}, u32[]{:S(2)}) copy-start(pred[8,1024]{1,0:T(8,128)(4,1)} %get-tuple-element.40) | copy-start | bytes 24580
  (8 other events, 16.6 us)
where the time goes:
time: 146 us
  local copies, waits for them, and re-layouts  66.6 us (46%)
  starting transfers between devices  57.3 us (39%)
  waiting for transfers between devices  13.6 us (9%)
  other arithmetic  7.52 us (5%)
    ppermute x12, starting transfers between devices, passed_along(): return lax.ppermute(block, axis, route)  57.3 us
    gather x2, local copies, waits for them, and re-layouts, on_device(): beside_all = jnp.take(extended, near_flat, axis=1, mode='clip')  14.8 us
    ppermute x12, waiting for transfers between devices, passed_along(): return lax.ppermute(block, axis, route)  13.6 us
    gather x1, local copies, waits for them, and re-layouts, on_device(): far_all = jnp.take(grad_extended, near_flat, axis=1, mode='clip')  12.6 us
    slice x4, local copies, waits for them, and re-layouts, on_device(): far_first = far_block[:row_count].reshape(shape_three)  11.8 us
    unnamed x67, local copies, waits for them, and re-layouts  9.2 us
    slice x3, local copies, waits for them, and re-layouts, on_device(): far_second = far_block[row_count:].reshape(shape_three)  5.96 us
    sub x1, other arithmetic, on_device(): return tracers - inv_mass * outflow  4.4 us
  transfers between devices with their start and end apart: 12, of which 2 were waited for; matrix products, arithmetic and copies ran while one was open for 7% of the time, Pallas kernels for 0%

commit v1 on v0

v1 whole, which is shorter than its diff:
```python
import functools

import jax
import jax.numpy as jnp
from jax import lax
from jax.experimental import pallas as pl
from jax.experimental.pallas import tpu as pltpu
from jax.sharding import PartitionSpec as P

LANES = 128
CHUNKS = 4


def peer_shift(peer_slot):
    return (peer_slot // 2 + 1) * (1 - 2 * (peer_slot % 2))


def lanes_of(row):
    wide = jnp.broadcast_to(row, (8, LANES))
    return jnp.bitwise_and(wide, LANES - 1), jnp.right_shift(wide, 7)


def taken(tile, lane):
    return jnp.take_along_axis(tile, lane, axis=1, mode="promise_in_bounds")


def kernel(
    device_count,
    x_any, flux_any, lsq_any, own_any, far_any, inv_any, near_any, send_any,
    out_any,
    x, flux, lsq, own, far, inv, near, send,
    value_out, value_in, grad_out, grad_in, grad, beside, early, result,
    load_sem, store_sem, value_send, value_recv, grad_send, grad_recv,
):
    me = lax.axis_index("dom")
    tracer_count, level_count, cell_count = x.shape
    peer_count = send.shape[0]
    tiles = cell_count // LANES
    step = tracer_count // CHUNKS
    targets = [
        lax.rem(me + peer_shift(slot) + device_count, device_count)
        for slot in range(peer_count)
    ]

    loads = []
    for slot, (source, target) in enumerate((
        (send_any, send), (x_any, x), (near_any, near), (lsq_any, lsq),
        (flux_any, flux), (own_any, own), (far_any, far), (inv_any, inv),
    )):
        copy = pltpu.make_async_copy(source, target, load_sem.at[slot])
        copy.start()
        loads.append(copy)

    barrier = pltpu.get_barrier_semaphore()
    for target in targets:
        pl.semaphore_signal(
            barrier, inc=1, device_id=(target,), device_id_type=pl.DeviceIdType.MESH
        )

    def cut(tile):
        return slice(tile * LANES, (tile + 1) * LANES)

    def value_copy(slot, chunk):
        part = pl.ds(chunk * step, step)
        return pltpu.make_async_remote_copy(
            src_ref=value_out.at[slot, part],
            dst_ref=value_in.at[slot, part],
            send_sem=value_send.at[slot, chunk],
            recv_sem=value_recv.at[slot, chunk],
            device_id=(targets[slot],),
            device_id_type=pl.DeviceIdType.MESH,
        )

    def grad_copy(slot, chunk):
        part = pl.ds(chunk * step, step)
        return pltpu.make_async_remote_copy(
            src_ref=grad_out.at[slot, part],
            dst_ref=grad_in.at[slot, part],
            send_sem=grad_send.at[slot, chunk],
            recv_sem=grad_recv.at[slot, chunk],
            device_id=(targets[slot],),
            device_id_type=pl.DeviceIdType.MESH,
        )

    def gather_values_to_send(chunk):
        for slot in range(peer_count):
            lane, tile = lanes_of(send[slot : slot + 1, :])
            for inner in range(step):
                t = chunk * step + inner
                found = taken(x[t, :, cut(0)], lane)
                for s in range(1, tiles):
                    found = jnp.where(tile == s, taken(x[t, :, cut(s)], lane), found)
                value_out[slot, t] = found

    def gather_own_values(chunk):
        for edge in range(3):
            for c in range(tiles):
                lane, tile = lanes_of(near[edge : edge + 1, cut(c)])
                for inner in range(step):
                    t = chunk * step + inner
                    found = taken(x[t, :, cut(0)], lane)
                    for s in range(1, tiles):
                        found = jnp.where(tile == s, taken(x[t, :, cut(s)], lane), found)
                    beside[edge, t, :, cut(c)] = found

    def make_gradients(chunk):
        for c in range(tiles):
            for inner in range(step):
                t = chunk * step + inner
                here = x[t, :, cut(c)]
                total = [None, None]
                for edge in range(3):
                    lane, tile = lanes_of(near[edge : edge + 1, cut(c)])
                    found = beside[edge, t, :, cut(c)]
                    for slot in range(peer_count):
                        found = jnp.where(
                            tile == tiles + slot, taken(value_in[slot, t], lane), found
                        )
                    beside[edge, t, :, cut(c)] = found
                    gap = found - here
                    for comp in range(2):
                        term = lsq[comp, edge : edge + 1, cut(c)] * gap
                        total[comp] = term if edge == 0 else total[comp] + term
                for comp in range(2):
                    grad[comp, t, :, cut(c)] = total[comp]

    def gather_gradients_to_send(chunk):
        for slot in range(peer_count):
            lane, tile = lanes_of(send[slot : slot + 1, :])
            for inner in range(step):
                t = chunk * step + inner
                for comp in range(2):
                    found = taken(grad[comp, t, :, cut(0)], lane)
                    for s in range(1, tiles):
                        found = jnp.where(
                            tile == s, taken(grad[comp, t, :, cut(s)], lane), found
                        )
                    grad_out[slot, t, comp] = found

    def make_early_faces(chunk):
        for edge in range(3):
            for c in range(tiles):
                lane, tile = lanes_of(near[edge : edge + 1, cut(c)])
                upwind = flux[edge, :, cut(c)] > 0
                for inner in range(step):
                    t = chunk * step + inner
                    slopes = []
                    for comp in range(2):
                        found = taken(grad[comp, t, :, cut(0)], lane)
                        for s in range(1, tiles):
                            found = jnp.where(
                                tile == s, taken(grad[comp, t, :, cut(s)], lane), found
                            )
                        slopes.append(found)
                    far_face = (
                        beside[edge, t, :, cut(c)]
                        + slopes[0] * far[0, edge, :, cut(c)]
                        + slopes[1] * far[1, edge, :, cut(c)]
                    )
                    own_face = (
                        x[t, :, cut(c)]
                        + grad[0, t, :, cut(c)] * own[0, edge, :, cut(c)]
                        + grad[1, t, :, cut(c)] * own[1, edge, :, cut(c)]
                    )
                    early[edge, t, :, cut(c)] = jnp.where(upwind, own_face, far_face)

    def finish(chunk):
        for c in range(tiles):
            for inner in range(step):
                t = chunk * step + inner
                here = x[t, :, cut(c)]
                outflow = None
                for edge in range(3):
                    lane, tile = lanes_of(near[edge : edge + 1, cut(c)])
                    side_flux = flux[edge, :, cut(c)]
                    late = jnp.logical_and(tile >= tiles, jnp.logical_not(side_flux > 0))
                    beyond = beside[edge, t, :, cut(c)]
                    slopes = []
                    for comp in range(2):
                        found = taken(grad_in[0, t, comp], lane)
                        for slot in range(1, peer_count):
                            found = jnp.where(
                                tile == tiles + slot, taken(grad_in[slot, t, comp], lane), found
                            )
                        slopes.append(found)
                    far_face = (
                        beyond
                        + slopes[0] * far[0, edge, :, cut(c)]
                        + slopes[1] * far[1, edge, :, cut(c)]
                    )
                    face = jnp.where(late, far_face, early[edge, t, :, cut(c)])
                    face = jnp.minimum(
                        jnp.maximum(face, jnp.minimum(here, beyond)), jnp.maximum(here, beyond)
                    )
                    term = side_flux * face
                    outflow = term if edge == 0 else outflow + term
                result[t, :, cut(c)] = here - inv[:, cut(c)] * outflow

    def over_chunks(body):
        lax.fori_loop(0, CHUNKS, lambda chunk, carry: (body(chunk), carry)[1], 0)

    loads[0].wait()
    loads[1].wait()
    over_chunks(gather_values_to_send)
    pl.semaphore_wait(barrier, peer_count)
    for chunk in range(CHUNKS):
        for slot in range(peer_count):
            value_copy(slot, chunk).start()
    for copy in loads[2:]:
        copy.wait()
    over_chunks(gather_own_values)

    def middle(chunk):
        for slot in range(peer_count):
            value_copy(slot, chunk).wait_recv()
        make_gradients(chunk)
        gather_gradients_to_send(chunk)
        for slot in range(peer_count):
            grad_copy(slot, chunk).start()

    over_chunks(middle)
    over_chunks(make_early_faces)

    def store(chunk):
        part = pl.ds(chunk * step, step)
        return pltpu.make_async_copy(result.at[part], out_any.at[part], store_sem.at[chunk])

    def last(chunk):
        for slot in range(peer_count):
            grad_copy(slot, chunk).wait_recv()
        finish(chunk)
        store(chunk).start()

    over_chunks(last)
    for chunk in range(CHUNKS):
        for slot in range(peer_count):
            value_copy(slot, chunk).wait_send()
            grad_copy(slot, chunk).wait_send()
        store(chunk).wait()


def on_device(
    device_count,
    tracers, mass_flux, lsq_coeff, own_offset, far_offset, inv_mass, neighbour, send_cells,
):
    tracer_count, level_count, cell_count = tracers.shape
    peer_count, halo_width = send_cells.shape
    f32 = jnp.float32
    arguments = (
        tracers, mass_flux, lsq_coeff, own_offset, far_offset, inv_mass, neighbour, send_cells,
    )
    halo = (peer_count, tracer_count, level_count, halo_width)
    halo_two = (peer_count, tracer_count, 2, level_count, halo_width)
    return pl.pallas_call(
        functools.partial(kernel, device_count),
        out_shape=jax.ShapeDtypeStruct(tracers.shape, f32),
        in_specs=[pl.BlockSpec(memory_space=pltpu.HBM)] * len(arguments),
        out_specs=pl.BlockSpec(memory_space=pltpu.HBM),
        scratch_shapes=[pltpu.VMEM(a.shape, a.dtype) for a in arguments]
        + [
            pltpu.VMEM(halo, f32),
            pltpu.VMEM(halo, f32),
            pltpu.VMEM(halo_two, f32),
            pltpu.VMEM(halo_two, f32),
            pltpu.VMEM((2, tracer_count, level_count, cell_count), f32),
            pltpu.VMEM((3, tracer_count, level_count, cell_count), f32),
            pltpu.VMEM((3, tracer_count, level_count, cell_count), f32),
            pltpu.VMEM(tracers.shape, f32),
            pltpu.SemaphoreType.DMA((len(arguments),)),
            pltpu.SemaphoreType.DMA((CHUNKS,)),
            pltpu.SemaphoreType.DMA((peer_count, CHUNKS)),
            pltpu.SemaphoreType.DMA((peer_count, CHUNKS)),
            pltpu.SemaphoreType.DMA((peer_count, CHUNKS)),
            pltpu.SemaphoreType.DMA((peer_count, CHUNKS)),
        ],
        compiler_params=pltpu.CompilerParams(collective_id=0, has_side_effects=True),
    )(*arguments)


def solution(mesh):
    placed = (
        P(None, None, "dom"),
        P(None, None, "dom"),
        P(None, None, "dom"),
        P(None, None, None, "dom"),
        P(None, None, None, "dom"),
        P(None, "dom"),
        P(None, "dom"),
        P(None, "dom"),
    )
    return jax.shard_map(
        functools.partial(on_device, mesh.shape["dom"]),
        mesh=mesh,
        in_specs=placed,
        out_specs=P(None, None, "dom"),
        check_vma=False,
    )
```

time: 146 us -> 49.8 us (0.34)
  the two profiles are of different devices: /device:TPU:247 before, /device:TPU:1 now
where the time goes in v1:
time: 49.8 us; the launch traced here: 49.5 us
  Pallas kernels  46.2 us (93%)
  local copies, waits for them, and re-layouts  3.35 us (7%)
    pallas_call x1, Pallas kernels, on_device(): pl.pallas_call(functools.partial(kernel, device_count), out_shape=jax.Sha...  46.2 us
    unnamed x2, local copies, waits for them, and re-layouts  3.35 us

profile of v1, /device:TPU:1, one launch (start us, length us, event | category | flops | bytes accessed | tf_op | source)
XLA Modules:
  0.0 49.5 jit_solution(8040287645495492543)
XLA Ops:
  0.0 1.4 %copy.9.lsq_any = f32[2,3,1024]{2,1,0:T(4,128)} copy(f32[2,3,1024]{2,0,1:T(2,128)} %param.10) | data formatting | bytes 49152 | tf_op args[2]
  1.4 46.2 %shard_map.82 = f32[20,8,1024]{2,1,0:T(8,128)} custom-call(f32[20,8,1024]{2,1,0:T(8,128)} %x_any.1, f32[3,8,1024]{2,1,0:T(8,128)} %flux_any.1, f32[2,3,1024]{2,1,0:T(4,128)} %copy.9.lsq_any, f32[2,3,8,1024]{3,2,1,0:T(8,128)} %own_any.1, f32[2,3,8,1024]{3,2,1,0:T(8,128)} %far_any.1, f32[8,1024]{1,0:T(8,128)} %inv_any.1, s32[3,1024]{1,0:T(4,128)} %near_any.1, ...), custom_call_target="tpu_custom_call" | custom-call | tf_op jit(solution)/shard_map/pallas_call | solution.py:254
  47.6 2.0 %copy.11 = f32[20,8,1024]{2,1,0:T(8,128)} copy(f32[20,8,1024]{2,1,0:T(8,128)} %shard_map.82) | data formatting | bytes 1310720

commit v2 on v1

--- a/solution.py
+++ b/solution.py
@@ -9,6 +9,7 @@
 
 LANES = 128
 CHUNKS = 4
+BLOCK = 256
 
 
 def peer_shift(peer_slot):
@@ -22,6 +23,11 @@
 
 def taken(tile, lane):
     return jnp.take_along_axis(tile, lane, axis=1, mode="promise_in_bounds")
+
+
+def in_two(value):
+    high = value.astype(jnp.bfloat16)
+    return high, (value - high.astype(jnp.float32)).astype(jnp.bfloat16)
 
 
 def kernel(
@@ -30,6 +36,7 @@
     out_any,
     x, flux, lsq, own, far, inv, near, send,
     value_out, value_in, grad_out, grad_in, grad, beside, early, result,
+    own_hot, halo_hot, value_split, grad_split, halo_split,
     load_sem, store_sem, value_send, value_recv, grad_send, grad_recv,
 ):
     me = lax.axis_index("dom")
@@ -92,16 +99,39 @@
                     found = jnp.where(tile == s, taken(x[t, :, cut(s)], lane), found)
                 value_out[slot, t] = found
 
-    def gather_own_values(chunk):
+    def split_values():
+        for t in range(0, tracer_count, 2):
+            rows = slice(t * level_count, (t + 2) * level_count)
+            for c in range(tiles):
+                pair = jnp.concatenate([x[t, :, cut(c)], x[t + 1, :, cut(c)]], axis=0)
+                for part, half in enumerate(in_two(pair)):
+                    value_split[part, rows, cut(c)] = half
+
+    def mark(hot, first):
+        depth = hot.shape[0]
         for edge in range(3):
-            for c in range(tiles):
-                lane, tile = lanes_of(near[edge : edge + 1, cut(c)])
-                for inner in range(step):
-                    t = chunk * step + inner
-                    found = taken(x[t, :, cut(0)], lane)
-                    for s in range(1, tiles):
-                        found = jnp.where(tile == s, taken(x[t, :, cut(s)], lane), found)
-                    beside[edge, t, :, cut(c)] = found
+            wanted = near[edge : edge + 1, :] - first
+            for k in range(0, depth, 256):
+                row = lax.broadcasted_iota(jnp.int32, (256, cell_count), 0) + k
+                hot[k : k + 256, edge * cell_count : (edge + 1) * cell_count] = jnp.where(
+                    row == wanted, 1.0, 0.0
+                ).astype(jnp.bfloat16)
+
+    def gathered(split, hot, edge, block):
+        rows = split.shape[1]
+        both = split[...].reshape(2 * rows, split.shape[2])
+        columns = pl.ds(
+            pl.multiple_of(edge * cell_count + block * BLOCK, BLOCK), BLOCK
+        )
+        found = jnp.dot(both, hot[:, columns], preferred_element_type=jnp.float32)
+        return found[:rows] + found[rows:]
+
+    def gather_own_values(edge):
+        for block in range(cell_count // BLOCK):
+            found = gathered(value_split, own_hot, edge, block)
+            beside[edge, :, :, slice(block * BLOCK, (block + 1) * BLOCK)] = found.reshape(
+                tracer_count, level_count, BLOCK
+            )
 
     def make_gradients(chunk):
         for c in range(tiles):
@@ -119,10 +149,13 @@
                     beside[edge, t, :, cut(c)] = found
                     gap = found - here
                     for comp in range(2):
-                        term = lsq[comp, edge : edge + 1, cut(c)] * gap
+                        term = lsq[edge, comp : comp + 1, cut(c)] * gap
                         total[comp] = term if edge == 0 else total[comp] + term
                 for comp in range(2):
                     grad[comp, t, :, cut(c)] = total[comp]
+                rows = pl.ds(pl.multiple_of(t * 2 * level_count, 2 * level_count), 2 * level_count)
+                for part, half in enumerate(in_two(jnp.concatenate(total, axis=0))):
+                    grad_split[part, rows, cut(c)] = half
 
     def gather_gradients_to_send(chunk):
         for slot in range(peer_count):
@@ -137,32 +170,57 @@
                         )
                     grad_out[slot, t, comp] = found
 
-    def make_early_faces(chunk):
-        for edge in range(3):
-            for c in range(tiles):
-                lane, tile = lanes_of(near[edge : edge + 1, cut(c)])
-                upwind = flux[edge, :, cut(c)] > 0
-                for inner in range(step):
-                    t = chunk * step + inner
-                    slopes = []
-                    for comp in range(2):
-                        found = taken(grad[comp, t, :, cut(0)], lane)
-                        for s in range(1, tiles):
-                            found = jnp.where(
-                                tile == s, taken(grad[comp, t, :, cut(s)], lane), found
-                            )
-                        slopes.append(found)
-                    far_face = (
-                        beside[edge, t, :, cut(c)]
-                        + slopes[0] * far[0, edge, :, cut(c)]
-                        + slopes[1] * far[1, edge, :, cut(c)]
+    def make_early_faces(edge):
+        for block in range(cell_count // BLOCK):
+            found = gathered(grad_split, own_hot, edge, block)
+            here = slice(block * BLOCK, (block + 1) * BLOCK)
+            upwind = flux[edge, :, here] > 0
+            for t in range(tracer_count):
+                top = t * 2 * level_count
+                first = found[top : top + level_count]
+                second = found[top + level_count : top + 2 * level_count]
+                far_face = (
+                    beside[edge, t, :, here]
+                    + first * far[0, edge, :, here]
+                    + second * far[1, edge, :, here]
+                )
+                own_face = (
+                    x[t, :, here]
+                    + grad[0, t, :, here] * own[0, edge, :, here]
+                    + grad[1, t, :, here] * own[1, edge, :, here]
+                )
+                early[edge, t, :, here] = jnp.where(upwind, own_face, far_face)
+
+    def add_halo_faces(chunk):
+        for inner in range(step):
+            t = chunk * step + inner
+            rows = slice(inner * 2 * level_count, (inner + 1) * 2 * level_count)
+            for slot in range(peer_count):
+                pair = grad_in[slot, t].reshape(2 * level_count, LANES)
+                for part, half in enumerate(in_two(pair)):
+                    halo_split[part, rows, cut(slot)] = half
+        for block in range(cell_count // BLOCK):
+            here = slice(block * BLOCK, (block + 1) * BLOCK)
+            slopes = [gathered(halo_split, halo_hot, edge, block) for edge in range(3)]
+            for inner in range(step):
+                t = chunk * step + inner
+                top = inner * 2 * level_count
+                center = x[t, :, here]
+                outflow = None
+                for edge in range(3):
+                    first = slopes[edge][top : top + level_count]
+                    second = slopes[edge][top + level_count : top + 2 * level_count]
+                    side_flux = flux[edge, :, here]
+                    beyond = beside[edge, t, :, here]
+                    extra = first * far[0, edge, :, here] + second * far[1, edge, :, here]
+                    face = early[edge, t, :, here] + jnp.where(side_flux > 0, 0.0, extra)
+                    face = jnp.minimum(
+                        jnp.maximum(face, jnp.minimum(center, beyond)),
+                        jnp.maximum(center, beyond),
                     )
-                    own_face = (
-                        x[t, :, cut(c)]
-                        + grad[0, t, :, cut(c)] * own[0, edge, :, cut(c)]
-                        + grad[1, t, :, cut(c)] * own[1, edge, :, cut(c)]
-                    )
-                    early[edge, t, :, cut(c)] = jnp.where(upwind, own_face, far_face)
+                    term = side_flux * face
+                    outflow = term if edge == 0 else outflow + term
+                result[t, :, here] = center - inv[:, here] * outflow
 
     def finish(chunk):
         for c in range(tiles):
@@ -196,19 +254,31 @@
                     outflow = term if edge == 0 else outflow + term
                 result[t, :, cut(c)] = here - inv[:, cut(c)] * outflow
 
-    def over_chunks(body):
-        lax.fori_loop(0, CHUNKS, lambda chunk, carry: (body(chunk), carry)[1], 0)
+    def over(count, body):
+        lax.fori_loop(0, count, lambda index, carry: (body(index), carry)[1], 0)
 
     loads[0].wait()
     loads[1].wait()
-    over_chunks(gather_values_to_send)
+    gather_values_to_send(0)
     pl.semaphore_wait(barrier, peer_count)
-    for chunk in range(CHUNKS):
+
+    def send_values(chunk):
         for slot in range(peer_count):
             value_copy(slot, chunk).start()
+
+    send_values(0)
+
+    def next_values(before):
+        gather_values_to_send(before + 1)
+        send_values(before + 1)
+
+    over(CHUNKS - 1, next_values)
     for copy in loads[2:]:
         copy.wait()
-    over_chunks(gather_own_values)
+    split_values()
+    mark(own_hot, 0)
+    over(3, gather_own_values)
+    mark(halo_hot, cell_count)
 
     def middle(chunk):
         for slot in range(peer_count):
@@ -218,20 +288,21 @@
         for slot in range(peer_count):
             grad_copy(slot, chunk).start()
 
-    over_chunks(middle)
-    over_chunks(make_early_faces)
+    over(CHUNKS, middle)
+    over(3, make_early_faces)
 
     def store(chunk):
         part = pl.ds(chunk * step, step)
         return pltpu.make_async_copy(result.at[part], out_any.at[part], store_sem.at[chunk])
 
-    def last(chunk):
+    def last(chunk, complete):
         for slot in range(peer_count):
             grad_copy(slot, chunk).wait_recv()
-        finish(chunk)
+        complete(chunk)
         store(chunk).start()
 
-    over_chunks(last)
+    over(CHUNKS - 1, lambda chunk: last(chunk, add_halo_faces))
+    last(CHUNKS - 1, finish)
     for chunk in range(CHUNKS):
         for slot in range(peer_count):
             value_copy(slot, chunk).wait_send()
@@ -245,9 +316,10 @@
 ):
     tracer_count, level_count, cell_count = tracers.shape
     peer_count, halo_width = send_cells.shape
-    f32 = jnp.float32
+    f32, bf16 = jnp.float32, jnp.bfloat16
     arguments = (
-        tracers, mass_flux, lsq_coeff, own_offset, far_offset, inv_mass, neighbour, send_cells,
+        tracers, mass_flux, lsq_coeff.transpose(1, 0, 2), own_offset, far_offset, inv_mass,
+        neighbour, send_cells,
     )
     halo = (peer_count, tracer_count, level_count, halo_width)
     halo_two = (peer_count, tracer_count, 2, level_count, halo_width)
@@ -266,6 +338,11 @@
             pltpu.VMEM((3, tracer_count, level_count, cell_count), f32),
             pltpu.VMEM((3, tracer_count, level_count, cell_count), f32),
             pltpu.VMEM(tracers.shape, f32),
+            pltpu.VMEM((cell_count, 3 * cell_count), bf16),
+            pltpu.VMEM((peer_count * halo_width, 3 * cell_count), bf16),
+            pltpu.VMEM((2, tracer_count * level_count, cell_count), bf16),
+            pltpu.VMEM((2, tracer_count * 2 * level_count, cell_count), bf16),
+            pltpu.VMEM((2, tracer_count // CHUNKS * 2 * level_count, peer_count * halo_width), bf16),
             pltpu.SemaphoreType.DMA((len(arguments),)),
             pltpu.SemaphoreType.DMA((CHUNKS,)),
             pltpu.SemaphoreType.DMA((peer_count, CHUNKS)),

time: 49.8 us -> 43.6 us (0.88)
  Pallas kernels: 46.2 us -> 41.5 us
  local copies, waits for them, and re-layouts: 3.35 us -> 1.99 us
    pallas_call x1, Pallas kernels: 46.2 us -> 41.5 us  [on_device(): pl.pallas_call(functools.partial(kernel, device_count), out_shape=jax.Sha...]
    unnamed x2 -> x1, local copies, waits for them, and re-layouts: 3.35 us -> 1.99 us
where the time goes in v2:
time: 43.6 us; the launch traced here: 43.5 us
  Pallas kernels  41.5 us (95%)
  local copies, waits for them, and re-layouts  1.99 us (5%)
    pallas_call x1, Pallas kernels, on_device(): pl.pallas_call(functools.partial(kernel, device_count), out_shape=jax.Sha...  41.5 us
    unnamed x1, local copies, waits for them, and re-layouts  1.99 us

profile of v2, /device:TPU:1, one launch (start us, length us, event | category | flops | bytes accessed | tf_op | source)
XLA Modules:
  0.0 43.5 jit_solution(9313515006259549312)
XLA Ops:
  0.0 41.5 %shard_map.82 = f32[20,8,1024]{2,1,0:T(8,128)} custom-call(f32[20,8,1024]{2,1,0:T(8,128)} %x_any.1, f32[3,8,1024]{2,1,0:T(8,128)} %flux_any.1, f32[3,2,1024]{2,1,0:T(2,128)} %bitcast.1, f32[2,3,8,1024]{3,2,1,0:T(8,128)} %own_any.1, f32[2,3,8,1024]{3,2,1,0:T(8,128)} %far_any.1, f32[8,1024]{1,0:T(8,128)} %inv_any.1, s32[3,1024]{1,0:T(4,128)} %near_any.1, ...), custom_call_target="tpu_custom_call" | custom-call | tf_op jit(solution)/shard_map/pallas_call | solution.py:326
  41.5 2.0 %copy.10 = f32[20,8,1024]{2,1,0:T(8,128)} copy(f32[20,8,1024]{2,1,0:T(8,128)} %shard_map.82) | data formatting | bytes 1310720

commit v3 on v2

--- a/solution.py
+++ b/solution.py
@@ -8,8 +8,10 @@
 from jax.sharding import PartitionSpec as P
 
 LANES = 128
-CHUNKS = 4
 BLOCK = 256
+PARTS = (2, 4, 6, 5, 3)
+JOINED = ((0, 1), (2,), (3,))
+ORDER = (4, 5, 2, 3, 0, 1)
 
 
 def peer_shift(peer_slot):
@@ -33,17 +35,17 @@
 def kernel(
     device_count,
     x_any, flux_any, lsq_any, own_any, far_any, inv_any, near_any, send_any,
-    out_any,
+    result,
     x, flux, lsq, own, far, inv, near, send,
-    value_out, value_in, grad_out, grad_in, grad, beside, early, result,
+    value_out, value_in, grad_out, grad_in, grad, beside, early,
     own_hot, halo_hot, value_split, grad_split, halo_split,
-    load_sem, store_sem, value_send, value_recv, grad_send, grad_recv,
+    load_sem, value_send, value_recv, grad_send, grad_recv,
 ):
     me = lax.axis_index("dom")
     tracer_count, level_count, cell_count = x.shape
     peer_count = send.shape[0]
     tiles = cell_count // LANES
-    step = tracer_count // CHUNKS
+    starts = [sum(PARTS[:chunk]) for chunk in range(len(PARTS) + 1)]
     targets = [
         lax.rem(me + peer_shift(slot) + device_count, device_count)
         for slot in range(peer_count)
@@ -51,7 +53,7 @@
 
     loads = []
     for slot, (source, target) in enumerate((
-        (send_any, send), (x_any, x), (near_any, near), (lsq_any, lsq),
+        (near_any, near), (send_any, send), (x_any, x), (lsq_any, lsq),
         (flux_any, flux), (own_any, own), (far_any, far), (inv_any, inv),
     )):
         copy = pltpu.make_async_copy(source, target, load_sem.at[slot])
@@ -68,7 +70,7 @@
         return slice(tile * LANES, (tile + 1) * LANES)
 
     def value_copy(slot, chunk):
-        part = pl.ds(chunk * step, step)
+        part = pl.ds(starts[chunk], PARTS[chunk])
         return pltpu.make_async_remote_copy(
             src_ref=value_out.at[slot, part],
             dst_ref=value_in.at[slot, part],
@@ -79,7 +81,7 @@
         )
 
     def grad_copy(slot, chunk):
-        part = pl.ds(chunk * step, step)
+        part = pl.ds(starts[chunk], PARTS[chunk])
         return pltpu.make_async_remote_copy(
             src_ref=grad_out.at[slot, part],
             dst_ref=grad_in.at[slot, part],
@@ -92,8 +94,7 @@
     def gather_values_to_send(chunk):
         for slot in range(peer_count):
             lane, tile = lanes_of(send[slot : slot + 1, :])
-            for inner in range(step):
-                t = chunk * step + inner
+            for t in range(starts[chunk], starts[chunk + 1]):
                 found = taken(x[t, :, cut(0)], lane)
                 for s in range(1, tiles):
                     found = jnp.where(tile == s, taken(x[t, :, cut(s)], lane), found)
@@ -110,33 +111,30 @@
     def mark(hot, first):
         depth = hot.shape[0]
         for edge in range(3):
-            wanted = near[edge : edge + 1, :] - first
+            wanted = (near[edge : edge + 1, :] - first).astype(jnp.int16)
             for k in range(0, depth, 256):
-                row = lax.broadcasted_iota(jnp.int32, (256, cell_count), 0) + k
+                row = lax.broadcasted_iota(jnp.int16, (256, cell_count), 0) + jnp.int16(k)
                 hot[k : k + 256, edge * cell_count : (edge + 1) * cell_count] = jnp.where(
-                    row == wanted, 1.0, 0.0
-                ).astype(jnp.bfloat16)
-
-    def gathered(split, hot, edge, block):
-        rows = split.shape[1]
-        both = split[...].reshape(2 * rows, split.shape[2])
-        columns = pl.ds(
-            pl.multiple_of(edge * cell_count + block * BLOCK, BLOCK), BLOCK
-        )
+                    row == wanted, jnp.bfloat16(1), jnp.bfloat16(0)
+                )
+
+    def gathered(split, rows, hot, edge, block):
+        both = jnp.concatenate([split[0, :rows], split[1, :rows]], axis=0)
+        first = edge * cell_count + block * BLOCK
+        columns = pl.ds(pl.multiple_of(first, BLOCK), BLOCK)
         found = jnp.dot(both, hot[:, columns], preferred_element_type=jnp.float32)
         return found[:rows] + found[rows:]
 
     def gather_own_values(edge):
         for block in range(cell_count // BLOCK):
-            found = gathered(value_split, own_hot, edge, block)
+            found = gathered(value_split, value_split.shape[1], own_hot, edge, block)
             beside[edge, :, :, slice(block * BLOCK, (block + 1) * BLOCK)] = found.reshape(
                 tracer_count, level_count, BLOCK
             )
 
     def make_gradients(chunk):
         for c in range(tiles):
-            for inner in range(step):
-                t = chunk * step + inner
+            for t in range(starts[chunk], starts[chunk + 1]):
                 here = x[t, :, cut(c)]
                 total = [None, None]
                 for edge in range(3):
@@ -153,15 +151,14 @@
                         total[comp] = term if edge == 0 else total[comp] + term
                 for comp in range(2):
                     grad[comp, t, :, cut(c)] = total[comp]
-                rows = pl.ds(pl.multiple_of(t * 2 * level_count, 2 * level_count), 2 * level_count)
+                rows = slice(t * 2 * level_count, (t + 1) * 2 * level_count)
                 for part, half in enumerate(in_two(jnp.concatenate(total, axis=0))):
                     grad_split[part, rows, cut(c)] = half
 
     def gather_gradients_to_send(chunk):
         for slot in range(peer_count):
             lane, tile = lanes_of(send[slot : slot + 1, :])
-            for inner in range(step):
-                t = chunk * step + inner
+            for t in range(starts[chunk], starts[chunk + 1]):
                 for comp in range(2):
                     found = taken(grad[comp, t, :, cut(0)], lane)
                     for s in range(1, tiles):
@@ -172,7 +169,7 @@
 
     def make_early_faces(edge):
         for block in range(cell_count // BLOCK):
-            found = gathered(grad_split, own_hot, edge, block)
+            found = gathered(grad_split, grad_split.shape[1], own_hot, edge, block)
             here = slice(block * BLOCK, (block + 1) * BLOCK)
             upwind = flux[edge, :, here] > 0
             for t in range(tracer_count):
@@ -191,19 +188,21 @@
                 )
                 early[edge, t, :, here] = jnp.where(upwind, own_face, far_face)
 
-    def add_halo_faces(chunk):
-        for inner in range(step):
-            t = chunk * step + inner
+    def add_halo_faces(first_tracer, count, blocks):
+        for inner in range(count):
             rows = slice(inner * 2 * level_count, (inner + 1) * 2 * level_count)
             for slot in range(peer_count):
-                pair = grad_in[slot, t].reshape(2 * level_count, LANES)
+                pair = grad_in[slot, first_tracer + inner].reshape(2 * level_count, LANES)
                 for part, half in enumerate(in_two(pair)):
                     halo_split[part, rows, cut(slot)] = half
-        for block in range(cell_count // BLOCK):
+        for block in blocks:
             here = slice(block * BLOCK, (block + 1) * BLOCK)
-            slopes = [gathered(halo_split, halo_hot, edge, block) for edge in range(3)]
-            for inner in range(step):
-                t = chunk * step + inner
+            slopes = [
+                gathered(halo_split, count * 2 * level_count, halo_hot, edge, block)
+                for edge in range(3)
+            ]
+            for inner in range(count):
+                t = first_tracer + inner
                 top = inner * 2 * level_count
                 center = x[t, :, here]
                 outflow = None
@@ -222,10 +221,9 @@
                     outflow = term if edge == 0 else outflow + term
                 result[t, :, here] = center - inv[:, here] * outflow
 
-    def finish(chunk):
-        for c in range(tiles):
-            for inner in range(step):
-                t = chunk * step + inner
+    def finish(chunk, columns):
+        for c in columns:
+            for t in range(starts[chunk], starts[chunk + 1]):
                 here = x[t, :, cut(c)]
                 outflow = None
                 for edge in range(3):
@@ -257,57 +255,47 @@
     def over(count, body):
         lax.fori_loop(0, count, lambda index, carry: (body(index), carry)[1], 0)
 
+    chunks = range(len(PARTS))
     loads[0].wait()
+    mark(own_hot, 0)
     loads[1].wait()
+    loads[2].wait()
     gather_values_to_send(0)
     pl.semaphore_wait(barrier, peer_count)
-
-    def send_values(chunk):
-        for slot in range(peer_count):
+    for chunk in chunks:
+        if chunk > 0:
+            gather_values_to_send(chunk)
+        for slot in ORDER:
             value_copy(slot, chunk).start()
-
-    send_values(0)
-
-    def next_values(before):
-        gather_values_to_send(before + 1)
-        send_values(before + 1)
-
-    over(CHUNKS - 1, next_values)
-    for copy in loads[2:]:
+    for copy in loads[3:]:
         copy.wait()
     split_values()
-    mark(own_hot, 0)
     over(3, gather_own_values)
-    mark(halo_hot, cell_count)
-
-    def middle(chunk):
-        for slot in range(peer_count):
+    for chunk in chunks:
+        for slot in ORDER:
             value_copy(slot, chunk).wait_recv()
         make_gradients(chunk)
         gather_gradients_to_send(chunk)
-        for slot in range(peer_count):
+        for slot in ORDER:
             grad_copy(slot, chunk).start()
-
-    over(CHUNKS, middle)
+    mark(halo_hot, cell_count)
     over(3, make_early_faces)
-
-    def store(chunk):
-        part = pl.ds(chunk * step, step)
-        return pltpu.make_async_copy(result.at[part], out_any.at[part], store_sem.at[chunk])
-
-    def last(chunk, complete):
-        for slot in range(peer_count):
-            grad_copy(slot, chunk).wait_recv()
-        complete(chunk)
-        store(chunk).start()
-
-    over(CHUNKS - 1, lambda chunk: last(chunk, add_halo_faces))
-    last(CHUNKS - 1, finish)
-    for chunk in range(CHUNKS):
-        for slot in range(peer_count):
+    blocks = range(cell_count // BLOCK)
+    for joined in JOINED:
+        for chunk in joined:
+            for slot in ORDER:
+                grad_copy(slot, chunk).wait_recv()
+        count = sum(PARTS[chunk] for chunk in joined)
+        add_halo_faces(starts[joined[0]], count, blocks)
+    final = len(PARTS) - 1
+    for slot in ORDER:
+        grad_copy(slot, final).wait_recv()
+    add_halo_faces(starts[final], PARTS[final], blocks[: len(blocks) // 2])
+    finish(final, range(tiles // 2, tiles))
+    for chunk in chunks:
+        for slot in ORDER:
             value_copy(slot, chunk).wait_send()
             grad_copy(slot, chunk).wait_send()
-        store(chunk).wait()
 
 
 def on_device(
@@ -327,7 +315,7 @@
         functools.partial(kernel, device_count),
         out_shape=jax.ShapeDtypeStruct(tracers.shape, f32),
         in_specs=[pl.BlockSpec(memory_space=pltpu.HBM)] * len(arguments),
-        out_specs=pl.BlockSpec(memory_space=pltpu.HBM),
+        out_specs=pl.BlockSpec(memory_space=pltpu.VMEM),
         scratch_shapes=[pltpu.VMEM(a.shape, a.dtype) for a in arguments]
         + [
             pltpu.VMEM(halo, f32),
@@ -337,21 +325,21 @@
             pltpu.VMEM((2, tracer_count, level_count, cell_count), f32),
             pltpu.VMEM((3, tracer_count, level_count, cell_count), f32),
             pltpu.VMEM((3, tracer_count, level_count, cell_count), f32),
-            pltpu.VMEM(tracers.shape, f32),
             pltpu.VMEM((cell_count, 3 * cell_count), bf16),
             pltpu.VMEM((peer_count * halo_width, 3 * cell_count), bf16),
             pltpu.VMEM((2, tracer_count * level_count, cell_count), bf16),
             pltpu.VMEM((2, tracer_count * 2 * level_count, cell_count), bf16),
-            pltpu.VMEM((2, tracer_count // CHUNKS * 2 * level_count, peer_count * halo_width), bf16),
+            pltpu.VMEM((2, 6 * 2 * level_count, peer_count * halo_width), bf16),
             pltpu.SemaphoreType.DMA((len(arguments),)),
-            pltpu.SemaphoreType.DMA((CHUNKS,)),
-            pltpu.SemaphoreType.DMA((peer_count, CHUNKS)),
-            pltpu.SemaphoreType.DMA((peer_count, CHUNKS)),
-            pltpu.SemaphoreType.DMA((peer_count, CHUNKS)),
-            pltpu.SemaphoreType.DMA((peer_count, CHUNKS)),
+            pltpu.SemaphoreType.DMA((peer_count, len(PARTS))),
+            pltpu.SemaphoreType.DMA((peer_count, len(PARTS))),
+            pltpu.SemaphoreType.DMA((peer_count, len(PARTS))),
+            pltpu.SemaphoreType.DMA((peer_count, len(PARTS))),
         ],
-        compiler_params=pltpu.CompilerParams(collective_id=0, has_side_effects=True),
-    )(*arguments)
+        compiler_params=pltpu.CompilerParams(
+            collective_id=0, has_side_effects=True, vmem_limit_bytes=48 * 1024 * 1024
+        ),
+    )(*[pltpu.with_memory_space_constraint(a, pltpu.HBM) for a in arguments])
 
 
 def solution(mesh):

time: 43.6 us -> 41.6 us (0.954)
  local copies, waits for them, and re-layouts: 1.99 us -> 0.84 us
  Pallas kernels: 41.5 us -> 40.5 us
    unnamed x1, local copies, waits for them, and re-layouts: 1.99 us -> 0.84 us
    pallas_call x1, Pallas kernels: 41.5 us -> 40.5 us  [on_device(): pl.pallas_call(functools.partial(kernel, device_count), out_shape=jax.Sha...]
where the time goes in v3:
time: 41.6 us; the launch traced here: 41.4 us
  Pallas kernels  40.5 us (97%)
  local copies, waits for them, and re-layouts  0.84 us (2%)
    pallas_call x1, Pallas kernels, on_device(): pl.pallas_call(functools.partial(kernel, device_count), out_shape=jax.Sha...  40.5 us
    unnamed x1, local copies, waits for them, and re-layouts  0.84 us

profile of v3, /device:TPU:1, one launch (start us, length us, event | category | flops | bytes accessed | tf_op | source)
XLA Modules:
  0.0 41.4 jit_solution(10675996747343803632)
XLA Ops:
  0.0 40.5 %shard_map.82 = f32[20,8,1024]{2,1,0:T(8,128)S(1)} custom-call(f32[20,8,1024]{2,1,0:T(8,128)} %x_any.1, f32[3,8,1024]{2,1,0:T(8,128)} %flux_any.1, f32[3,2,1024]{2,1,0:T(2,128)} %bitcast.1, f32[2,3,8,1024]{3,2,1,0:T(8,128)} %own_any.1, f32[2,3,8,1024]{3,2,1,0:T(8,128)} %far_any.1, f32[8,1024]{1,0:T(8,128)} %inv_any.1, s32[3,1024]{1,0:T(4,128)} %near_any.1, ...), custom_call_target="tpu_custom_call" | custom-call | tf_op jit(solution)/shard_map/pallas_call | solution.py:314
  40.5 0.8 %copy.10 = f32[20,8,1024]{2,1,0:T(8,128)} copy(f32[20,8,1024]{2,1,0:T(8,128)S(1)} %shard_map.82) | data formatting | bytes 1310720

commit v4 on v3

--- a/solution.py
+++ b/solution.py
@@ -9,8 +9,9 @@
 
 LANES = 128
 BLOCK = 256
-PARTS = (2, 4, 6, 5, 3)
-JOINED = ((0, 1), (2,), (3,))
+PARTS = (2, 3, 5, 7, 3)
+SENT = (2, 3, 5, 7, 3)
+JOINED = (((0, 1), 3), ((2,), 3), ((3,), 3), ((4,), 2))
 ORDER = (4, 5, 2, 3, 0, 1)
 
 
@@ -46,25 +47,26 @@
     peer_count = send.shape[0]
     tiles = cell_count // LANES
     starts = [sum(PARTS[:chunk]) for chunk in range(len(PARTS) + 1)]
+    cuts = [sum(SENT[:piece]) for piece in range(len(SENT) + 1)]
     targets = [
         lax.rem(me + peer_shift(slot) + device_count, device_count)
         for slot in range(peer_count)
     ]
 
+    barrier = pltpu.get_barrier_semaphore()
+    for target in targets:
+        pl.semaphore_signal(
+            barrier, inc=1, device_id=(target,), device_id_type=pl.DeviceIdType.MESH
+        )
+
     loads = []
     for slot, (source, target) in enumerate((
-        (near_any, near), (send_any, send), (x_any, x), (lsq_any, lsq),
+        (send_any, send), (x_any, x), (near_any, near), (lsq_any, lsq),
         (flux_any, flux), (own_any, own), (far_any, far), (inv_any, inv),
     )):
         copy = pltpu.make_async_copy(source, target, load_sem.at[slot])
         copy.start()
         loads.append(copy)
-
-    barrier = pltpu.get_barrier_semaphore()
-    for target in targets:
-        pl.semaphore_signal(
-            barrier, inc=1, device_id=(target,), device_id_type=pl.DeviceIdType.MESH
-        )
 
     def cut(tile):
         return slice(tile * LANES, (tile + 1) * LANES)
@@ -80,13 +82,13 @@
             device_id_type=pl.DeviceIdType.MESH,
         )
 
-    def grad_copy(slot, chunk):
-        part = pl.ds(starts[chunk], PARTS[chunk])
+    def grad_copy(slot, piece):
+        part = pl.ds(cuts[piece], SENT[piece])
         return pltpu.make_async_remote_copy(
             src_ref=grad_out.at[slot, part],
             dst_ref=grad_in.at[slot, part],
-            send_sem=grad_send.at[slot, chunk],
-            recv_sem=grad_recv.at[slot, chunk],
+            send_sem=grad_send.at[slot, piece],
+            recv_sem=grad_recv.at[slot, piece],
             device_id=(targets[slot],),
             device_id_type=pl.DeviceIdType.MESH,
         )
@@ -133,26 +135,28 @@
             )
 
     def make_gradients(chunk):
+        members = range(starts[chunk], starts[chunk + 1])
         for c in range(tiles):
-            for t in range(starts[chunk], starts[chunk + 1]):
-                here = x[t, :, cut(c)]
-                total = [None, None]
-                for edge in range(3):
-                    lane, tile = lanes_of(near[edge : edge + 1, cut(c)])
+            total = {}
+            for edge in range(3):
+                lane, tile = lanes_of(near[edge : edge + 1, cut(c)])
+                for t in members:
                     found = beside[edge, t, :, cut(c)]
                     for slot in range(peer_count):
                         found = jnp.where(
                             tile == tiles + slot, taken(value_in[slot, t], lane), found
                         )
                     beside[edge, t, :, cut(c)] = found
-                    gap = found - here
+                    gap = found - x[t, :, cut(c)]
                     for comp in range(2):
                         term = lsq[edge, comp : comp + 1, cut(c)] * gap
-                        total[comp] = term if edge == 0 else total[comp] + term
+                        total[t, comp] = term if edge == 0 else total[t, comp] + term
+            for t in members:
+                pair = [total[t, comp] for comp in range(2)]
                 for comp in range(2):
-                    grad[comp, t, :, cut(c)] = total[comp]
+                    grad[comp, t, :, cut(c)] = pair[comp]
                 rows = slice(t * 2 * level_count, (t + 1) * 2 * level_count)
-                for part, half in enumerate(in_two(jnp.concatenate(total, axis=0))):
+                for part, half in enumerate(in_two(jnp.concatenate(pair, axis=0))):
                     grad_split[part, rows, cut(c)] = half
 
     def gather_gradients_to_send(chunk):
@@ -221,15 +225,16 @@
                     outflow = term if edge == 0 else outflow + term
                 result[t, :, here] = center - inv[:, here] * outflow
 
-    def finish(chunk, columns):
+    def finish(first_tracer, count, columns):
+        members = range(first_tracer, first_tracer + count)
         for c in columns:
-            for t in range(starts[chunk], starts[chunk + 1]):
-                here = x[t, :, cut(c)]
-                outflow = None
-                for edge in range(3):
-                    lane, tile = lanes_of(near[edge : edge + 1, cut(c)])
-                    side_flux = flux[edge, :, cut(c)]
-                    late = jnp.logical_and(tile >= tiles, jnp.logical_not(side_flux > 0))
+            outflow = {}
+            for edge in range(3):
+                lane, tile = lanes_of(near[edge : edge + 1, cut(c)])
+                side_flux = flux[edge, :, cut(c)]
+                late = jnp.logical_and(tile >= tiles, jnp.logical_not(side_flux > 0))
+                for t in members:
+                    here = x[t, :, cut(c)]
                     beyond = beside[edge, t, :, cut(c)]
                     slopes = []
                     for comp in range(2):
@@ -249,17 +254,16 @@
                         jnp.maximum(face, jnp.minimum(here, beyond)), jnp.maximum(here, beyond)
                     )
                     term = side_flux * face
-                    outflow = term if edge == 0 else outflow + term
-                result[t, :, cut(c)] = here - inv[:, cut(c)] * outflow
+                    outflow[t] = term if edge == 0 else outflow[t] + term
+            for t in members:
+                result[t, :, cut(c)] = x[t, :, cut(c)] - inv[:, cut(c)] * outflow[t]
 
     def over(count, body):
         lax.fori_loop(0, count, lambda index, carry: (body(index), carry)[1], 0)
 
-    chunks = range(len(PARTS))
+    chunks, pieces = range(len(PARTS)), range(len(SENT))
     loads[0].wait()
-    mark(own_hot, 0)
     loads[1].wait()
-    loads[2].wait()
     gather_values_to_send(0)
     pl.semaphore_wait(barrier, peer_count)
     for chunk in chunks:
@@ -267,8 +271,9 @@
             gather_values_to_send(chunk)
         for slot in ORDER:
             value_copy(slot, chunk).start()
-    for copy in loads[3:]:
+    for copy in loads[2:]:
         copy.wait()
+    mark(own_hot, 0)
     split_values()
     over(3, gather_own_values)
     for chunk in chunks:
@@ -276,26 +281,24 @@
             value_copy(slot, chunk).wait_recv()
         make_gradients(chunk)
         gather_gradients_to_send(chunk)
-        for slot in ORDER:
-            grad_copy(slot, chunk).start()
+        for piece in pieces:
+            if starts[chunk] <= cuts[piece] < starts[chunk + 1]:
+                for slot in ORDER:
+                    grad_copy(slot, piece).start()
     mark(halo_hot, cell_count)
     over(3, make_early_faces)
-    blocks = range(cell_count // BLOCK)
-    for joined in JOINED:
-        for chunk in joined:
+    for joined, by_matmul in JOINED:
+        for piece in joined:
             for slot in ORDER:
-                grad_copy(slot, chunk).wait_recv()
-        count = sum(PARTS[chunk] for chunk in joined)
-        add_halo_faces(starts[joined[0]], count, blocks)
-    final = len(PARTS) - 1
+                grad_copy(slot, piece).wait_recv()
+        count = sum(SENT[piece] for piece in joined)
+        add_halo_faces(cuts[joined[0]], count, range(by_matmul))
+        finish(cuts[joined[0]], count, range(by_matmul * BLOCK // LANES, tiles))
     for slot in ORDER:
-        grad_copy(slot, final).wait_recv()
-    add_halo_faces(starts[final], PARTS[final], blocks[: len(blocks) // 2])
-    finish(final, range(tiles // 2, tiles))
-    for chunk in chunks:
-        for slot in ORDER:
+        for chunk in chunks:
             value_copy(slot, chunk).wait_send()
-            grad_copy(slot, chunk).wait_send()
+        for piece in pieces:
+            grad_copy(slot, piece).wait_send()
 
 
 def on_device(
@@ -329,12 +332,12 @@
             pltpu.VMEM((peer_count * halo_width, 3 * cell_count), bf16),
             pltpu.VMEM((2, tracer_count * level_count, cell_count), bf16),
             pltpu.VMEM((2, tracer_count * 2 * level_count, cell_count), bf16),
-            pltpu.VMEM((2, 6 * 2 * level_count, peer_count * halo_width), bf16),
+            pltpu.VMEM((2, 7 * 2 * level_count, peer_count * halo_width), bf16),
             pltpu.SemaphoreType.DMA((len(arguments),)),
             pltpu.SemaphoreType.DMA((peer_count, len(PARTS))),
             pltpu.SemaphoreType.DMA((peer_count, len(PARTS))),
-            pltpu.SemaphoreType.DMA((peer_count, len(PARTS))),
-            pltpu.SemaphoreType.DMA((peer_count, len(PARTS))),
+            pltpu.SemaphoreType.DMA((peer_count, len(SENT))),
+            pltpu.SemaphoreType.DMA((peer_count, len(SENT))),
         ],
         compiler_params=pltpu.CompilerParams(
             collective_id=0, has_side_effects=True, vmem_limit_bytes=48 * 1024 * 1024

time: 41.6 us -> 40.9 us (0.983)
  Pallas kernels: 40.5 us -> 39.9 us
    pallas_call x1, Pallas kernels: 40.5 us -> 39.9 us  [on_device(): pl.pallas_call(functools.partial(kernel, device_count), out_shape=jax.Sha...]
where the time goes in v4:
time: 40.9 us; the launch traced here: 40.8 us
  Pallas kernels  39.9 us (98%)
  local copies, waits for them, and re-layouts  0.84 us (2%)
    pallas_call x1, Pallas kernels, on_device(): pl.pallas_call(functools.partial(kernel, device_count), out_shape=jax.Sha...  39.9 us
    unnamed x1, local copies, waits for them, and re-layouts  0.84 us

profile of v4, /device:TPU:1, one launch (start us, length us, event | category | flops | bytes accessed | tf_op | source)
XLA Modules:
  0.0 40.8 jit_solution(724990167850270204)
XLA Ops:
  0.0 39.9 %shard_map.82 = f32[20,8,1024]{2,1,0:T(8,128)S(1)} custom-call(f32[20,8,1024]{2,1,0:T(8,128)} %x_any.1, f32[3,8,1024]{2,1,0:T(8,128)} %flux_any.1, f32[3,2,1024]{2,1,0:T(2,128)} %bitcast.1, f32[2,3,8,1024]{3,2,1,0:T(8,128)} %own_any.1, f32[2,3,8,1024]{3,2,1,0:T(8,128)} %far_any.1, f32[8,1024]{1,0:T(8,128)} %inv_any.1, s32[3,1024]{1,0:T(4,128)} %near_any.1, ...), custom_call_target="tpu_custom_call" | custom-call | tf_op jit(solution)/shard_map/pallas_call | solution.py:317
  39.9 0.8 %copy.10 = f32[20,8,1024]{2,1,0:T(8,128)} copy(f32[20,8,1024]{2,1,0:T(8,128)S(1)} %shard_map.82) | data formatting | bytes 1310720

commit v5 on v4

--- a/solution.py
+++ b/solution.py
@@ -9,10 +9,10 @@
 
 LANES = 128
 BLOCK = 256
-PARTS = (2, 3, 5, 7, 3)
+PARTS = (2, 3, 5, 10)
 SENT = (2, 3, 5, 7, 3)
 JOINED = (((0, 1), 3), ((2,), 3), ((3,), 3), ((4,), 2))
-ORDER = (4, 5, 2, 3, 0, 1)
+ORDER = (2, 3, 0, 1, 4, 5)
 
 
 def peer_shift(peer_slot):

time: 40.9 us -> 40.8 us (level)
  no operation moved by 1% of the time
where the time goes in v5:
time: 40.8 us; the launch traced here: 40.7 us
  Pallas kernels  39.8 us (98%)
  local copies, waits for them, and re-layouts  0.84 us (2%)
    pallas_call x1, Pallas kernels, on_device(): pl.pallas_call(functools.partial(kernel, device_count), out_shape=jax.Sha...  39.8 us
    unnamed x1, local copies, waits for them, and re-layouts  0.84 us

profile of v5, /device:TPU:1, one launch (start us, length us, event | category | flops | bytes accessed | tf_op | source)
XLA Modules:
  0.0 40.7 jit_solution(10389041263415357235)
XLA Ops:
  0.0 39.8 %shard_map.82 = f32[20,8,1024]{2,1,0:T(8,128)S(1)} custom-call(f32[20,8,1024]{2,1,0:T(8,128)} %x_any.1, f32[3,8,1024]{2,1,0:T(8,128)} %flux_any.1, f32[3,2,1024]{2,1,0:T(2,128)} %bitcast.1, f32[2,3,8,1024]{3,2,1,0:T(8,128)} %own_any.1, f32[2,3,8,1024]{3,2,1,0:T(8,128)} %far_any.1, f32[8,1024]{1,0:T(8,128)} %inv_any.1, s32[3,1024]{1,0:T(4,128)} %near_any.1, ...), custom_call_target="tpu_custom_call" | custom-call | tf_op jit(solution)/shard_map/pallas_call | solution.py:317
  39.8 0.8 %copy.10 = f32[20,8,1024]{2,1,0:T(8,128)} copy(f32[20,8,1024]{2,1,0:T(8,128)S(1)} %shard_map.82) | data formatting | bytes 1310720
